TPU v7x, 256 devices: a whole 4x4x8 slice. The times are simulated.
256 devices in a mesh: batch: 8 (over z), mp: 32 (over x, y, core).
Axes of the slice: x: 4, y: 4, z: 8, core: 2. Of those that a mesh axis runs over, the one named last changes fastest.
Arguments:
- stream: bfloat16 [256, 8192], P(None, 'mp'), may hold values from -6 to 6
- input_gain: float32 [8192], P('mp'), may hold values from 0.5 to 1.5
- query_bias: float32 [8192], P('batch'), may hold values from -3 to 3
- query_weight: bfloat16 [8192, 8192], P('mp', 'batch'), may hold values from -0.0625 to 0.0625
- out_weight: bfloat16 [8192, 8192], P('batch', 'mp'), may hold values from -6 to 6
- page_cache: bfloat16 [2, 8, 2048, 128, 128], P(None, 'batch', 'mp'), may hold values from -43 to 43
- page_table: int32 [256, 24], P('mp'), may hold values from 0 to 63, as said below
- lengths: int32 [256], P('mp'), may hold values from 1 to 3072, as said below
- final_gain: float32 [8192], P('mp'), may hold values from 0.5 to 1.5
- head_weight: bfloat16 [8192, 98304], P('mp', 'batch'), may hold values from -11 to 11
Outputs:
- logits: float32 [256, 98304], P(None, ('batch', 'mp'))
- log_norm: float32 [256], replicated
Inputs may be any that keep to these rules, and one draw needn't show every extreme that they name: Each sequence's pages are the first ceil(lengths / 128) entries of its row of page_table; together the sequences of one index of mp use at most 64 pages; some sequence holds exactly 3072 tokens. `page_table`: entries are slots of the pool of the index of mp that holds the sequence; the live entries (the first ceil(lengths / 128) of each row) of all rows of one index of mp are distinct; later entries are arbitrary slots.
All inputs are finite; a program needn't handle non-finite values.
Results may differ from a plain program's by a relative error of at most 0.0099.
Values may be sent and summed in bfloat16 or wider, within the bound.
No kernel may reach another device: no remote copies, remote signals or barrier semaphores. Data moves between devices by JAX's collectives and lax.ppermute only.
A program may use at most 128 MiB of HBM per device.

v0:
```python
import functools
import math

import jax
import jax.numpy as jnp
from jax import lax
from jax.experimental import pallas as pl
from jax.experimental.pallas import tpu as pltpu
from jax.sharding import Mesh
from jax.sharding import PartitionSpec as P

MP = ("mp_0", "mp_1", "mp_2")
BATCH_MP = ("batch", "mp_0", "mp_1", "mp_2")
XY = ("mp_0", "mp_1")
BATCH_CORE = ("batch", "mp_2")


EPS = 1e-06
ROPE_BASE = 1000000.0
INTERPRET = False

LANES = 128
HEAD_VMEM = 24 * 2**20
ATTEND_VMEM = 16 * 2**20


def near_by(x):
    return pltpu.with_memory_space_constraint(x, pltpu.VMEM)


def far_off(x):
    return pltpu.with_memory_space_constraint(x, pltpu.HBM)


def sent_to_all(x, axis):
    length = lax.axis_size(axis)
    return lax.all_to_all(jnp.broadcast_to(x[None], (length, *x.shape)), axis, 0, 0, tiled=True)


def shifted(x, axis, by):
    length = lax.axis_size(axis)
    return lax.ppermute(x, axis, [(k, (k + by) % length) for k in range(length)])


def query_block(stream, gain, weight, out):
    width = weight.shape[1]
    features = stream[...].astype(jnp.float32)
    squares = jnp.sum(features * features, axis=1, keepdims=True)
    products = jnp.dot(
        (features * gain[...]).astype(jnp.bfloat16), weight[...], preferred_element_type=jnp.float32
    )
    out[:, :width] = products.astype(jnp.bfloat16)
    coarse = squares.astype(jnp.bfloat16).astype(jnp.float32)
    lane = lax.broadcasted_iota(jnp.int32, (features.shape[0], LANES), 1)
    tail = jnp.where(lane == 0, coarse, jnp.where(lane == 1, squares - coarse, 0.0))
    out[:, width:] = tail.astype(jnp.bfloat16)


def query_parts(stream, gain, weight):
    return pl.pallas_call(
        query_block,
        out_shape=pltpu.VMEM((stream.shape[0], weight.shape[1] + LANES), jnp.bfloat16),
        interpret=INTERPRET,
        name="query_parts",
    )(stream, gain[None], weight)


def turns(position, head_size):
    half_dim = head_size // 2
    exponent = jnp.arange(half_dim, dtype=jnp.float32) * (-2.0 / head_size)
    frequency = ROPE_BASE**exponent
    angles = position.astype(jnp.float32)[:, None] * frequency[None, :]
    cosines, sines = jnp.cos(angles), jnp.sin(angles)
    return (
        jnp.concatenate([cosines, cosines], axis=1),
        jnp.concatenate([-sines, sines], axis=1),
    )


def token_owners(page_table, lengths, pool_size, page_size):
    seq_count, max_pages = page_table.shape
    page_order = jnp.arange(max_pages, dtype=jnp.int32)
    used_pages = (lengths + page_size - 1) // page_size
    slot_ids = jnp.arange(pool_size, dtype=jnp.int32)
    matches = (page_table[:, :, None] == slot_ids[None, None, :]) & (
        page_order[None, :, None] < used_pages[:, None, None]
    )
    seq_ids = jnp.arange(seq_count, dtype=jnp.int32)
    owner = jnp.sum(jnp.where(matches, seq_ids[:, None, None], 0), axis=(0, 1))
    remaining = lengths[:, None] - page_order[None, :] * page_size
    visible = jnp.sum(jnp.where(matches, remaining[:, :, None], 0), axis=(0, 1))
    at = jnp.arange(page_size, dtype=jnp.int32)
    return jnp.where(at[None, :] < visible[:, None], owner[:, None], -1)


def attend_block(full_width, chunks, sums, table, owners, pages, out, *scratch):
    keys, values, scores, sems = scratch
    copies, seq_count, width = out.shape
    pool_size, page_size, head_size = keys.shape
    heads = width // head_size
    rows = heads * seq_count
    fetched = pool_size // sems.shape[1]
    slots = pool_size // chunks
    tokens = slots * page_size

    fetches = []
    for kind, held in enumerate((keys, values)):
        for k in range(pool_size // fetched):
            at = pl.ds(k * fetched, fetched)
            copy = pltpu.make_async_copy(pages.at[kind, 0, at], held.at[at], sems.at[kind, k])
            copy.start()
            fetches.append(copy)

    bias, cosines = table[:, :width], table[:, width : width + head_size]
    sines = table[:, width + head_size :]
    tail = sums[:, width:]
    lane = lax.broadcasted_iota(jnp.int32, tail.shape, 1)
    squares = jnp.sum(jnp.where(lane < 2, tail, 0.0), axis=1, keepdims=True)
    turned = sums[:, :width] * lax.rsqrt(squares / full_width + EPS) + bias
    pieces = []
    for k in range(heads):
        piece = turned[:, k * head_size : (k + 1) * head_size]
        across = pltpu.roll(piece, head_size // 2, 1)
        pieces.append(piece * cosines + across * sines)
    queries = jnp.concatenate(pieces, axis=0).astype(jnp.bfloat16)

    row_seq = lax.broadcasted_iota(jnp.int32, (rows, 1), 0) % seq_count
    highest = jnp.full((rows, head_size), -1e30, jnp.float32)
    for k in range(chunks):
        if k * slots % fetched == 0:
            fetches[k * slots // fetched].wait()
        key = keys[k * slots : (k + 1) * slots].reshape(tokens, head_size)
        here = lax.dot_general(
            queries, key, (((1,), (1,)), ((), ())), preferred_element_type=jnp.float32
        ) * (1.0 / math.sqrt(head_size))
        at = slice(k * tokens, (k + 1) * tokens)
        here = jnp.where(owners[:, at] == row_seq, here, -1e30)
        scores[:, at] = here
        for t in range(tokens // head_size):
            highest = jnp.maximum(highest, here[:, t * head_size : (t + 1) * head_size])
    highest = jnp.max(highest, axis=1, keepdims=True)
    summed = jnp.zeros((rows, head_size), jnp.float32)
    mixed = jnp.zeros((rows, head_size), jnp.float32)
    for k in range(chunks):
        powers = jnp.exp(scores[:, k * tokens : (k + 1) * tokens] - highest)
        for t in range(tokens // head_size):
            summed += powers[:, t * head_size : (t + 1) * head_size]
        if k * slots % fetched == 0:
            fetches[pool_size // fetched + k * slots // fetched].wait()
        value = values[k * slots : (k + 1) * slots].reshape(tokens, head_size)
        mixed += jnp.dot(powers.astype(jnp.bfloat16), value, preferred_element_type=jnp.float32)
    result = mixed / jnp.sum(summed, axis=1, keepdims=True)
    row = [result[k * seq_count : (k + 1) * seq_count] for k in range(heads)]
    row = jnp.concatenate(row, axis=1).astype(jnp.bfloat16)
    for k in range(copies):
        out[k] = row


def attend(sums, table, owners, page_cache, full_width, copies, fetches=1, chunks=4):
    seq_count, width = sums.shape
    width -= LANES
    pool_size, page_size, head_size = page_cache.shape[2:]
    pool = (pool_size, page_size, head_size)
    rows = width // head_size * seq_count
    in_hbm = pl.BlockSpec(memory_space=pltpu.HBM)
    in_vmem = pl.BlockSpec(memory_space=pltpu.VMEM)
    return pl.pallas_call(
        functools.partial(attend_block, full_width, chunks),
        in_specs=[in_vmem, in_vmem, in_vmem, in_hbm],
        out_specs=in_vmem,
        out_shape=pltpu.VMEM((copies, seq_count, width), jnp.bfloat16),
        scratch_shapes=[
            pltpu.VMEM(pool, jnp.bfloat16),
            pltpu.VMEM(pool, jnp.bfloat16),
            pltpu.VMEM((rows, pool_size * page_size), jnp.float32),
            pltpu.SemaphoreType.DMA((2, fetches)),
        ],
        compiler_params=pltpu.CompilerParams(vmem_limit_bytes=ATTEND_VMEM),
        interpret=INTERPRET,
        name="attend",
    )(near_by(sums), near_by(table), near_by(owners.reshape(1, -1)), far_off(page_cache))


def in_order(gathered):
    batches, cores, per_batch, _, _ = gathered.shape
    pieces = [
        gathered[b, c, i].astype(jnp.float32)
        for b in range(batches)
        for i in range(per_batch)
        for c in range(cores)
    ]
    return jnp.concatenate(pieces, axis=0)


def squares_line(rows, gain):
    unscaled = rows * (1.0 / gain)
    squares = jnp.sum(unscaled * unscaled, axis=1, keepdims=True)
    shape = (rows.shape[0], rows.shape[0])
    diagonal = lax.broadcasted_iota(jnp.int32, shape, 0) == lax.broadcasted_iota(jnp.int32, shape, 1)
    return jnp.sum(jnp.where(diagonal, squares, 0.0), axis=0, keepdims=True)


def head_block(place, gathered, gain, near_weight, far_weight, *refs):
    _, cores, _, _, depth = gathered.shape
    side = len(refs) // 2
    out_x, out_y = refs[: side - 1], refs[side - 1 : 2 * side - 2]
    weights, sems_in = refs[2 * side - 2 :]
    held = [k for k in range(side) if k != side // 2]
    x_at, y_at, core_at = place[0], place[1], place[2]
    width = near_weight.shape[1] // (side * side * cores)
    rows_here = depth // cores

    def weight_copies(x_to, y_to):
        column = (((x_at + x_to) % side) * side + (y_at + y_to) % side) * cores + core_at
        column = pl.multiple_of(column * width, width)
        copies = []
        for k, (weight, core) in enumerate(((near_weight, core_at), (far_weight, 1 - core_at))):
            row = pl.multiple_of(core * rows_here, rows_here)
            copies.append(
                pltpu.make_async_copy(
                    weight.at[:, pl.ds(column, width)],
                    weights.at[x_to, pl.ds(row, rows_here), pl.ds(y_to * width, width)],
                    sems_in.at[x_to, y_to * 2 + k],
                )
            )
        return copies

    loads = [[c for y_to in range(side) for c in weight_copies(x_to, y_to)] for x_to in range(side)]
    for copies in loads:
        for copy in copies:
            copy.start()

    ordered = in_order(gathered)
    features = ordered.astype(jnp.bfloat16)
    half = ordered.shape[0] // 2
    extra = out_x[0].shape[1] - half
    tails = []
    for part in (ordered[:half], ordered[half:]):
        line = jnp.broadcast_to(squares_line(part, gain[...]), (extra, half))
        coarse = line.astype(jnp.bfloat16)
        fine = (line - coarse.astype(jnp.float32)).astype(jnp.bfloat16)
        filler = jnp.zeros((extra, width - 2 * half), jnp.bfloat16)
        tails.append(jnp.concatenate([coarse, fine, filler], axis=1))
    tail_x, tail_y = tails

    for x_to in range(side):
        for copy in loads[x_to]:
            copy.wait()
        product = jnp.dot(features, weights[x_to], preferred_element_type=jnp.float32)
        for y_to in range(side):
            part = product[:, y_to * width : (y_to + 1) * width].astype(jnp.bfloat16)
            if x_to in held:
                out_x[held.index(x_to)][y_to, :half] = part[:half]
                out_x[held.index(x_to)][y_to, half:] = tail_x
            if y_to in held:
                out_y[held.index(y_to)][x_to, :half] = part[half:]
                out_y[held.index(y_to)][x_to, half:] = tail_y


def head_partials(gathered, gain, near_weight, far_weight, place, side):
    batches, cores, per_batch, seq_count, depth = gathered.shape
    half = batches * cores * per_batch * seq_count // 2
    width = near_weight.shape[1] // (side * side * cores)
    block = (side, half + 8, width)
    in_hbm = pl.BlockSpec(memory_space=pltpu.HBM)
    outs = pl.pallas_call(
        head_block,
        in_specs=[
            pl.BlockSpec(memory_space=pltpu.SMEM),
            pl.BlockSpec(memory_space=pltpu.VMEM),
            pl.BlockSpec(memory_space=pltpu.VMEM),
            in_hbm,
            in_hbm,
        ],
        out_shape=[pltpu.VMEM(block, jnp.bfloat16)] * (2 * side - 2),
        scratch_shapes=[
            pltpu.VMEM((side, depth, side * width), jnp.bfloat16),
            pltpu.SemaphoreType.DMA((side, 2 * side)),
        ],
        compiler_params=pltpu.CompilerParams(vmem_limit_bytes=HEAD_VMEM),
        interpret=INTERPRET,
        name="head_partials",
    )(
        place,
        near_by(gathered),
        near_by(gain),
        far_off(near_weight),
        far_off(far_weight),
    )
    return outs[: side - 1], outs[side - 1 :]


def partner_weights_block(sizes, place, near_weight, far_weight, out_x, out_y, held, sems, sems_out):
    side, cores, width = sizes
    rows_here = near_weight.shape[0]
    x_at, y_at, core_at = place[0], place[1], place[2]
    copies = []
    for t in range(side):
        places = (
            ((x_at + side // 2) % side, (y_at + t) % side),
            ((x_at + t) % side, (y_at + side // 2) % side),
        )
        for way, (x_to, y_to) in enumerate(places):
            column = pl.multiple_of(((x_to * side + y_to) * cores + core_at) * width, width)
            for k, weight in enumerate((near_weight, far_weight)):
                copy = pltpu.make_async_copy(
                    weight.at[:, pl.ds(column, width)],
                    held.at[way, pl.ds(k * rows_here, rows_here), pl.ds(t * width, width)],
                    sems.at[way, k, t],
                )
                copy.start()
                copies.append(copy)
    for copy in copies:
        copy.wait()
    stores = [
        pltpu.make_async_copy(held.at[way], out, sems_out.at[way])
        for way, out in enumerate((out_x, out_y))
    ]
    for copy in stores:
        copy.start()
    for copy in stores:
        copy.wait()


def partner_weights(near_weight, far_weight, place, side, cores):
    rows_here, columns = near_weight.shape
    width = columns // (side * side * cores)
    shape = (cores * rows_here, side * width)
    in_hbm = pl.BlockSpec(memory_space=pltpu.HBM)
    return pl.pallas_call(
        functools.partial(partner_weights_block, (side, cores, width)),
        in_specs=[pl.BlockSpec(memory_space=pltpu.SMEM), in_hbm, in_hbm],
        out_specs=[in_hbm, in_hbm],
        out_shape=[pltpu.HBM(shape, jnp.bfloat16)] * 2,
        scratch_shapes=[
            pltpu.VMEM((2, *shape), jnp.bfloat16),
            pltpu.SemaphoreType.DMA((2, cores, side)),
            pltpu.SemaphoreType.DMA((2,)),
        ],
        compiler_params=pltpu.CompilerParams(vmem_limit_bytes=ATTEND_VMEM),
        interpret=INTERPRET,
        name="partner_weights",
    )(place, far_off(near_weight), far_off(far_weight))


def head_partner_block(core, rows_x, rows_y, gain_x, gain_y, weight_x, weight_y, *outs):
    weights = (weight_x, weight_y)
    rows_here = rows_x.shape[-1] // 2
    first_core = core[0] == 0
    for way, (rows, gain) in enumerate(((rows_x, gain_x), (rows_y, gain_y))):
        side, tall, width = outs[way].shape
        ordered = in_order(rows)
        half = ordered.shape[0]
        line = jnp.broadcast_to(squares_line(ordered, gain[...]), (tall - half, half))
        tail = jnp.concatenate(
            [line, jnp.zeros((tall - half, width - half), jnp.float32)], axis=1
        )
        sides = (ordered[:, :rows_here], ordered[:, rows_here:])
        near = jnp.where(first_core, sides[0], sides[1])
        far = jnp.where(first_core, sides[1], sides[0])
        features = jnp.concatenate([near, far], axis=1).astype(jnp.bfloat16)
        product = jnp.dot(features, weights[way][...], preferred_element_type=jnp.float32)
        for t in range(side):
            outs[way][t, :half] = product[:, t * width : (t + 1) * width]
            outs[way][t, half:] = tail


def head_partner(rows_x, rows_y, gain_x, gain_y, weight_x, weight_y, core_at, side):
    depth, columns = weight_x.shape
    half = rows_x.size // depth
    block = (side, half + 8, columns // side)
    in_vmem = pl.BlockSpec(memory_space=pltpu.VMEM)
    return pl.pallas_call(
        head_partner_block,
        in_specs=[pl.BlockSpec(memory_space=pltpu.SMEM), *[in_vmem] * 6],
        out_shape=[pltpu.VMEM(block, jnp.float32)] * 2,
        compiler_params=pltpu.CompilerParams(vmem_limit_bytes=ATTEND_VMEM),
        interpret=INTERPRET,
        name="head_partner",
    )(
        core_at.astype(jnp.int32)[None],
        *(near_by(x) for x in (rows_x, rows_y, gain_x, gain_y, weight_x, weight_y)),
    )


def summed_along(parts, axis):
    arrived = [shifted(parts[k], axis, k) for k in range(1, len(parts))]
    total = parts[0].astype(jnp.float32)
    for piece in arrived:
        total = total + piece.astype(jnp.float32)
    return total


def summed_near(parts, partner, axis):
    side = lax.axis_size(axis)
    arrived = [shifted(parts[-1 if k > 1 else 1], axis, k) for k in (1, side - 1)]
    total = parts[0].astype(jnp.float32) + partner
    for piece in arrived:
        total = total + piece.astype(jnp.float32)
    return total


def joined_all(top, total, axes):
    for axis in axes:
        pieces = sent_to_all(jnp.stack([top, total]), axis)
        tops = pieces[:, 0]
        top = jnp.max(tops, axis=0)
        total = jnp.sum(pieces[:, 1] * jnp.exp(tops - top[None]), axis=0)
    return top, total


def local(
    stream,
    input_gain,
    query_bias,
    query_weight,
    out_weight,
    page_cache,
    page_table,
    lengths,
    final_gain,
    head_weight,
):
    side, cores, batches = lax.axis_size("mp_0"), lax.axis_size("mp_2"), lax.axis_size("batch")
    members = side * side * cores
    x_at, y_at, core_at = lax.axis_index("mp_0"), lax.axis_index("mp_1"), lax.axis_index("mp_2")
    batch_at = lax.axis_index("batch")
    first_core = core_at == 0
    seqs, features_here = stream.shape
    full_width = features_here * members
    seq_count = page_table.shape[0]
    head_size = page_cache.shape[-1]

    far_head_weight = shifted(head_weight, "mp_2", 1)
    far_out_weight = shifted(out_weight, "mp_2", 1)

    parts = query_parts(stream, input_gain, query_weight).reshape(members, seq_count, -1)
    parts = lax.all_to_all(parts, MP, split_axis=0, concat_axis=0, tiled=True)
    owners = token_owners(page_table, lengths, *page_cache.shape[2:4])
    cosines, sines = turns(lengths - 1, head_size)
    bias = jnp.broadcast_to(query_bias[None], (seq_count, query_bias.shape[0]))
    table = jnp.concatenate([bias, cosines, sines], axis=1)
    sums = jnp.sum(parts.astype(jnp.float32), axis=0)
    attended = attend(
        sums, table, owners, page_cache, full_width, side * side
    )

    mine = lax.all_to_all(attended, XY, 0, 0, tiled=True)
    place = jnp.stack([x_at, y_at, core_at]).astype(jnp.int32)
    weight_x, weight_y = partner_weights(head_weight, far_head_weight, place, side, cores)
    weight_x = shifted(weight_x, "mp_0", side // 2)
    weight_y = shifted(weight_y, "mp_1", side // 2)
    mine = mine.reshape(side * side * seq_count, -1)
    near_out = jnp.dot(mine, out_weight, preferred_element_type=jnp.float32)
    far_out = jnp.dot(mine, far_out_weight, preferred_element_type=jnp.float32)
    partial_out = jnp.concatenate(
        [jnp.where(first_core, near_out, far_out), jnp.where(first_core, far_out, near_out)], axis=1
    ).astype(jnp.bfloat16)
    per_batch = side * side // batches
    arrived = lax.all_to_all(
        partial_out.reshape(batches, per_batch * seq_count, -1),
        "batch",
        split_axis=0,
        concat_axis=0,
        tiled=True,
    )
    rows = stream.reshape(batches, per_batch, cores, seq_count, features_here)
    rows = lax.dynamic_index_in_dim(rows, batch_at, 0, keepdims=False)

    def of_core(core):
        taken = lax.dynamic_index_in_dim(rows, core, 1, keepdims=False).reshape(-1, features_here)
        return jnp.concatenate([taken.astype(jnp.float32), final_gain[None]], axis=0)

    near_rows = of_core(core_at)
    far_rows = shifted(of_core(1 - core_at), "mp_2", 1)
    both = jnp.concatenate(
        [jnp.where(first_core, near_rows, far_rows), jnp.where(first_core, far_rows, near_rows)],
        axis=1,
    )
    residual = both[:-1] + jnp.sum(arrived.astype(jnp.float32), axis=0)
    payload = (residual * both[-1:]).astype(jnp.bfloat16)
    gathered = sent_to_all(payload, BATCH_CORE)
    gathered = gathered.reshape(batches, cores, per_batch, seq_count, -1)
    rows_x = shifted(gathered[: batches // 2], "mp_0", side // 2)
    rows_y = shifted(gathered[batches // 2 :], "mp_1", side // 2)
    gain = both[-1:]
    gain_x = shifted(gain, "mp_0", side // 2)
    gain_y = shifted(gain, "mp_1", side // 2)
    upper, lower = head_partials(gathered, gain, head_weight, far_head_weight, place, side)
    partner_x, partner_y = head_partner(
        rows_x, rows_y, gain_x, gain_y, weight_x, weight_y, core_at, side
    )
    upper = summed_near(upper, partner_x, "mp_0").astype(jnp.bfloat16)
    lower = summed_near(lower, partner_y, "mp_1").astype(jnp.bfloat16)
    upper = summed_along([upper[k] for k in range(side)], "mp_1")
    lower = summed_along([lower[k] for k in range(side)], "mp_0")

    def rescaled(total):
        half = seqs // 2
        squares = total[half, :half] + total[half, half : 2 * half]
        return total[:half] * lax.rsqrt(squares / full_width + EPS)[:, None]

    logits = jnp.concatenate([rescaled(upper), rescaled(lower)], axis=0)

    local_top = jnp.max(logits, axis=1)
    local_sum = jnp.sum(jnp.exp(logits - local_top[:, None]), axis=1)
    highest, summed = joined_all(local_top, local_sum, (MP, "batch"))
    return (logits, jnp.log(summed) + highest)


def solution(mesh):
    torus = Mesh(
        mesh.devices.reshape(mesh.shape["batch"], 4, 4, 2), ("batch", "mp_0", "mp_1", "mp_2")
    )
    in_specs = (
        P(None, MP),
        P(MP),
        P("batch"),
        P(MP, "batch"),
        P("batch", MP),
        P(None, "batch", MP, None, None),
        P(MP, None),
        P(MP),
        P(MP),
        P(MP, "batch"),
    )
    out_specs = (P(None, BATCH_MP), P())

    def step(*args):
        return local(*args)

    step = jax.shard_map(step, mesh=torus, in_specs=in_specs, out_specs=out_specs, check_vma=False)
    return step
```

profile of v0, /device:TPU:1, one launch (start us, length us, event | category | flops | bytes accessed | tf_op | source)
XLA Modules:
  0.0 158.6 jit_solution(1225260360534017877)
XLA Ops:
  0.7 3.3 %collective-permute-start.2 = (bf16[256,12288]{1,0:T(8,128)(2,1)}, bf16[256,12288]{1,0:T(8,128)(2,1)}, u32[]{:S(2)}, u32[]{:S(2)}) collective-permute-start(bf16[256,12288]{1,0:T(8,128)(2,1)} %near_weight.3), channel_id=1, source_target_pairs={{0,1},{1,0},{2,3},{3,2},{4,5},{5,4},{6,7},{7,6},{8,9},{9,8},{10,11... | collective-permute-start | bytes 18874376 | tf_op jit(solution)/shard_map/ppermute | solution.py:42
  4.0 2.3 %query_parts.1 = bf16[256,1152]{1,0:T(8,128)(2,1)} custom-call(bf16[256,256]{1,0:T(8,128)(2,1)} %stream.1, f32[1,256]{1,0:T(1,128)} %bitcast.101, bf16[256,1024]{1,0:T(8,128)(2,1)} %weight.1), custom_call_target="tpu_custom_call" | custom-call | tf_op jit(solution)/shard_map/query_parts/pallas_call | solution.py:60
  6.2 5.5 %all-to-all-start = ((bf16[32,8,1152]{2,1,0:T(8,128)(2,1)}), bf16[32,8,1152]{2,1,0:T(8,128)(2,1)S(1)}, u32[]{:S(2)}, u32[]{:S(2)}) async-start(bf16[32,8,1152]{2,1,0:T(8,128)(2,1)} %bitcast.8), calls=%async_computation | async-start | bytes 1179648 | tf_op jit(solution)/shard_map/all_to_all | solution.py:438
  11.7 0.3 collective-permute-start.1
  12.1 0.1 iota_compare_fusion.2
  12.2 0.1 multiply_sine_fusion
  12.3 0.1 concatenate.27.table
  12.4 0.1 broadcast_subtract_fusion
  12.5 0.2 select_reduce_fusion.1
  12.6 0.1 fusion.17
  12.7 11.3 %all-to-all-done = bf16[32,8,1152]{2,1,0:T(8,128)(2,1)S(1)} async-done(((bf16[32,8,1152]{2,1,0:T(8,128)(2,1)}), bf16[32,8,1152]{2,1,0:T(8,128)(2,1)S(1)}, u32[]{:S(2)}, u32[]{:S(2)}) %all-to-all-start) | async-done | bytes 589856 | tf_op jit(solution)/shard_map/all_to_all | solution.py:438
  24.0 0.1 convert_reduce_fusion.sums
  24.1 3.8 %attend.1 = bf16[16,8,1024]{2,1,0:T(8,128)(2,1)} custom-call(f32[8,1152]{1,0:T(8,128)S(1)} %convert_reduce_fusion.sums, f32[8,1280]{1,0:T(8,128)S(1)} %concatenate.27.table, s32[1,8192]{1,0:T(1,128)S(1)} %bitcast.88, bf16[2,1,64,128,128]{4,3,2,1,0:T(8,128)(2,1)} %pages.1), custom_call_target="tpu_custom_call" | custom-call | tf_op jit(solution)/shard_map/attend/pallas_call | solution.py:167
  27.9 3.5 %all-to-all-start.1 = ((bf16[16,8,1024]{2,1,0:T(8,128)(2,1)}), bf16[16,8,1024]{2,1,0:T(8,128)(2,1)S(1)}, u32[]{:S(2)}, u32[]{:S(2)}) async-start(bf16[16,8,1024]{2,1,0:T(8,128)(2,1)} %attend.1), calls=%async_computation.1 | async-start | bytes 524288 | tf_op jit(solution)/shard_map/all_to_all | solution.py:448
  31.5 0.7 bitcast_convert_fusion.1
  32.2 0.2 collective-permute-start
  32.4 0.1 pad_add_fusion.place
  32.4 6.9 %all-to-all-done.1 = bf16[16,8,1024]{2,1,0:T(8,128)(2,1)S(1)} async-done(((bf16[16,8,1024]{2,1,0:T(8,128)(2,1)}), bf16[16,8,1024]{2,1,0:T(8,128)(2,1)S(1)}, u32[]{:S(2)}, u32[]{:S(2)}) %all-to-all-start.1) | async-done | bytes 262176 | tf_op jit(solution)/shard_map/all_to_all | solution.py:448
  39.3 0.2 fusion.2
  39.6 0.2 select_convert_fusion.1
  39.8 0.7 pad_maximum_fusion.1
  40.5 8.2 %all-to-all-start.2 = ((bf16[8,16,512]{2,1,0:T(8,128)(2,1)}), bf16[8,16,512]{2,1,0:T(8,128)(2,1)S(1)}, u32[]{:S(2)}, u32[]{:S(2)}) async-start(bf16[8,16,512]{2,1,0:T(8,128)(2,1)} %pad_maximum_fusion.1), calls=%async_computation.2 | async-start | bytes 262144 | tf_op jit(solution)/shard_map/all_to_all | solution.py:460
  48.7 4.4 %partner_weights.1 = (bf16[512,1536]{1,0:T(8,128)(2,1)}, bf16[512,1536]{1,0:T(8,128)(2,1)}) custom-call(s32[3]{0:T(128)S(1)} %pad_add_fusion.place, bf16[256,12288]{1,0:T(8,128)(2,1)} %near_weight.3, bf16[256,12288]{1,0:T(8,128)(2,1)} %collective-permute-done.2.far_weight), custom_call_target="tpu_custom_call" | custom-call | tf_op jit(solution)/shard_map/partner_weights/pallas_call | solution.py:330
  53.1 1.4 collective-permute-start.7
  54.5 1.5 collective-permute-start.8
  56.0 0.6 all-to-all-done.2
  56.7 0.7 broadcast_in_dim.54
  57.4 8.4 %all-to-all-start.3 = ((bf16[16,16,512]{2,1,0:T(8,128)(2,1)}), bf16[16,16,512]{2,1,0:T(8,128)(2,1)S(1)}, u32[]{:S(2)}, u32[]{:S(2)}) async-start(bf16[16,16,512]{2,1,0:T(8,128)(2,1)} %broadcast_in_dim.54), calls=%async_computation.3 | async-start | bytes 524288 | tf_op jit(solution)/shard_map/all_to_all | solution.py:37
  65.8 1.9 %collective-permute-start.5 = (f32[1,512]{1,0:T(1,128)S(1)}, f32[1,512]{1,0:T(1,128)S(1)}, u32[]{:S(2)}, u32[]{:S(2)}) collective-permute-start(f32[1,512]{1,0:T(1,128)S(1)} %pad_maximum_fusion.4.gain), channel_id=1, source_target_pairs={{0,16},{8,24},{16,0},{24,8},{1,17},{9,25},{17,1},{25,9},{2,18},{10... | collective-permute-start | bytes 6152 | tf_op jit(solution)/shard_map/ppermute | solution.py:42
  67.7 1.8 %collective-permute-start.6 = (f32[1,512]{1,0:T(1,128)S(1)}, f32[1,512]{1,0:T(1,128)S(1)}, u32[]{:S(2)}, u32[]{:S(2)}) collective-permute-start(f32[1,512]{1,0:T(1,128)S(1)} %pad_maximum_fusion.4.gain), channel_id=1, source_target_pairs={{0,4},{2,6},{4,0},{6,2},{1,5},{3,7},{5,1},{7,3},{8,12},{10,14},{12... | collective-permute-start | bytes 6152 | tf_op jit(solution)/shard_map/ppermute | solution.py:42
  69.5 7.9 %all-to-all-done.3 = bf16[16,16,512]{2,1,0:T(8,128)(2,1)S(1)} async-done(((bf16[16,16,512]{2,1,0:T(8,128)(2,1)}), bf16[16,16,512]{2,1,0:T(8,128)(2,1)S(1)}, u32[]{:S(2)}, u32[]{:S(2)}) %all-to-all-start.3) | async-done | bytes 262176 | tf_op jit(solution)/shard_map/all_to_all | solution.py:37
  77.4 4.8 %head_partials.1 = (bf16[4,136,384]{2,1,0:T(8,128)(2,1)S(1)}, bf16[4,136,384]{2,1,0:T(8,128)(2,1)S(1)}, bf16[4,136,384]{2,1,0:T(8,128)(2,1)S(1)}, bf16[4,136,384...) custom-call(s32[3]{0:T(128)S(1)} %pad_add_fusion.place, ...), custom_call_target="tpu_custom_call" | custom-call | tf_op jit(solution)/shard_map/head_partials/pallas_call | solution.py:266
  82.2 1.5 collective-permute-start.10
  83.7 5.4 %collective-permute-done.5.gain_x = f32[1,512]{1,0:T(1,128)S(1)} collective-permute-done((f32[1,512]{1,0:T(1,128)S(1)}, f32[1,512]{1,0:T(1,128)S(1)}, u32[]{:S(2)}, u32[]{:S(2)}) %collective-permute-start.5) | collective-permute-done | bytes 2080 | tf_op jit(solution)/shard_map/ppermute | solution.py:42
  89.1 0.1 collective-permute-start.9
  89.2 1.2 collective-permute-done.6.gain_y
  90.4 1.8 %collective-permute-start.3 = (bf16[4,2,2,8,512]{4,3,2,1,0:T(8,128)(2,1)S(1)}, bf16[4,2,2,8,512]{4,3,2,1,0:T(8,128)(2,1)S(1)}, u32[]{:S(2)}, u32[]{:S(2)}) collective-permute-start(bf16[4,2,2,8,512]{4,3,2,1,0:T(8,128)(2,1)S(1)} %bitcast.94), channel_id=1, source_target_pairs={{0,16},{8,24},{16,0},{24,8},{1,17},{9,25},{17,1},{25,9},{2,18},{10... | collective-permute-start | bytes 393224 | tf_op jit(solution)/shard_map/ppermute | solution.py:42
  92.2 8.2 %collective-permute-done.3.rows_x = bf16[4,2,2,8,512]{4,3,2,1,0:T(8,128)(2,1)S(1)} collective-permute-done((bf16[4,2,2,8,512]{4,3,2,1,0:T(8,128)(2,1)S(1)}, bf16[4,2,2,8,512]{4,3,2,1,0:T(8,128)(2,1)S(1)}, u32[]{:S(2)}, u32[]{:S(2)}) %collective-permute-start.3) | collective-permute-done | bytes 131104 | tf_op jit(solution)/shard_map/ppermute | solution.py:42
  100.5 5.3 %collective-permute-done.4.rows_y = bf16[4,2,2,8,512]{4,3,2,1,0:T(8,128)(2,1)S(1)} collective-permute-done((bf16[4,2,2,8,512]{4,3,2,1,0:T(8,128)(2,1)S(1)}, bf16[4,2,2,8,512]{4,3,2,1,0:T(8,128)(2,1)S(1)}, u32[]{:S(2)}, u32[]{:S(2)}) %collective-permute-start.4) | collective-permute-done | bytes 131104 | tf_op jit(solution)/shard_map/ppermute | solution.py:42
  105.8 0.4 collective-permute-start.14
  106.1 2.3 %collective-permute-start.15 = (bf16[4,136,384]{2,1,0:T(8,128)(2,1)S(1)}, bf16[4,136,384]{2,1,0:T(8,128)(2,1)S(1)}, u32[]{:S(2)}, u32[]{:S(2)}) collective-permute-start(bf16[4,136,384]{2,1,0:T(8,128)(2,1)S(1)} %get-tuple-element.21), channel_id=1, source_target_pairs={{0,6},{2,0},{4,2},{6,4},{1,7},{3,1},{5,3},{7,5},{8,14},{10,8},{12,... | collective-permute-start | bytes 1253384 | tf_op jit(solution)/shard_map/ppermute | solution.py:42
  108.5 0.6 head_partner.1
  109.1 0.2 add_convert_fusion.1
  109.3 0.1 collective-permute-start.11
  109.4 1.2 collective-permute-start.12
  110.6 1.5 collective-permute-start.13
  112.1 3.2 %collective-permute-done.14 = bf16[4,136,384]{2,1,0:T(8,128)(2,1)S(1)} collective-permute-done((bf16[4,136,384]{2,1,0:T(8,128)(2,1)S(1)}, bf16[4,136,384]{2,1,0:T(8,128)(2,1)S(1)}, u32[]{:S(2)}, u32[]{:S(2)}) %collective-permute-start.14) | collective-permute-done | bytes 417824 | tf_op jit(solution)/shard_map/ppermute | solution.py:42
  115.3 0.2 add_convert_fusion
  115.5 0.1 collective-permute-start.16
  115.6 2.4 %collective-permute-start.17 = (bf16[136,384]{1,0:T(8,128)(2,1)S(1)}, bf16[136,384]{1,0:T(8,128)(2,1)S(1)}, u32[]{:S(2)}, u32[]{:S(2)}) collective-permute-start(bf16[136,384]{1,0:T(8,128)(2,1)S(1)} %get-tuple-element.31), channel_id=1, source_target_pairs={{0,16},{8,24},{16,0},{24,8},{1,17},{9,25},{17,1},{25,9},{2,18},{10... | collective-permute-start | bytes 313352 | tf_op jit(solution)/shard_map/ppermute | solution.py:42
  118.0 1.2 collective-permute-start.18
  119.2 0.1 fusion.7
  119.3 0.1 slice_multiply_fusion.1
  119.4 2.4 %collective-permute-done.16 = bf16[136,384]{1,0:T(8,128)(2,1)S(1)} collective-permute-done((bf16[136,384]{1,0:T(8,128)(2,1)S(1)}, bf16[136,384]{1,0:T(8,128)(2,1)S(1)}, u32[]{:S(2)}, u32[]{:S(2)}) %collective-permute-start.16) | collective-permute-done | bytes 104480 | tf_op jit(solution)/shard_map/ppermute | solution.py:42
  121.8 0.6 collective-permute-done.18
  122.3 0.1 fusion.5
  122.4 0.1 slice_multiply_fusion
  122.5 0.1 fusion.26
  122.6 0.0 copy-start
  122.6 0.2 exponential_reduce_fusion
  122.9 22.1 %all_to_all.30 = f32[32,2,256]{2,1,0:T(2,128)S(1)} all-to-all(f32[32,2,256]{2,1,0:T(2,128)S(1)} %broadcast_in_dim.55), channel_id=1, replica_groups=mesh['batch'=8,'mp_0'=4,'mp_1'=4,'mp_2'=2] {'mp_0','mp_1','mp_2'}, dimensions={0} | all-to-all | bytes 131072 | tf_op jit(solution)/shard_map/all_to_all | solution.py:37
  145.0 0.1 slice_reduce_fusion.1
  145.2 12.8 %all_to_all.31 = f32[8,2,256]{2,1,0:T(2,128)S(1)} all-to-all(f32[8,2,256]{2,1,0:T(2,128)S(1)} %broadcast_in_dim.56), channel_id=1, replica_groups=mesh['batch'=8,'mp_0'=4,'mp_1'=4,'mp_2'=2] {'batch'}, dimensions={0} | all-to-all | bytes 32768 | tf_op jit(solution)/shard_map/all_to_all | solution.py:37
  158.0 0.6 log_add_fusion
  (45 shorter events, 0.4 us)
Async XLA Ops:
  0.6 11.1 %copy-start.1 = (bf16[1024,256]{1,0:T(8,128)(2,1)S(1)}, bf16[1024,256]{1,0:T(8,128)(2,1)}, u32[]{:S(2)}) copy-start(bf16[1024,256]{1,0:T(8,128)(2,1)} %param.14) | copy-start | bytes 1572868
  0.6 11.4 %copy-start.5 = (s32[8]{0:T(128)S(1)}, s32[8]{0:T(128)}, u32[]{:S(2)}) copy-start(s32[8]{0:T(128)} %param.17) | copy-start | bytes 100
  0.7 11.6 %copy-start.2 = (f32[1024]{0:T(1024)S(1)}, f32[1024]{0:T(1024)}, u32[]{:S(2)}) copy-start(f32[1024]{0:T(1024)} %param.12) | copy-start | bytes 12292
  0.7 11.8 %copy-start.4 = (s32[8,24]{1,0:T(8,128)S(1)}, s32[8,24]{1,0:T(8,128)}, u32[]{:S(2)}) copy-start(s32[8,24]{1,0:T(8,128)} %param.16) | copy-start | bytes 2308
  0.7 48.0 %collective-permute-start.2 = (bf16[256,12288]{1,0:T(8,128)(2,1)}, bf16[256,12288]{1,0:T(8,128)(2,1)}, u32[]{:S(2)}, u32[]{:S(2)}) collective-permute-start(bf16[256,12288]{1,0:T(8,128)(2,1)} %near_weight.3), channel_id=1, source_target_pairs={{0,1},{1,0},{2,3},{3,2},{4,5},{5,4},{6,7},{7,6},{8,9},{9,8},{10,11... | collective-permute-start | bytes 18874376 | tf_op jit(solution)/shard_map/ppermute | solution.py:42
  6.2 17.8 %all-to-all-start = ((bf16[32,8,1152]{2,1,0:T(8,128)(2,1)}), bf16[32,8,1152]{2,1,0:T(8,128)(2,1)S(1)}, u32[]{:S(2)}, u32[]{:S(2)}) async-start(bf16[32,8,1152]{2,1,0:T(8,128)(2,1)} %bitcast.8), calls=%async_computation | async-start | bytes 1179648 | tf_op jit(solution)/shard_map/all_to_all | solution.py:438
  11.7 27.9 %collective-permute-start.1 = (bf16[1024,256]{1,0:T(8,128)(2,1)S(1)}, bf16[1024,256]{1,0:T(8,128)(2,1)S(1)}, u32[]{:S(2)}, u32[]{:S(2)}) collective-permute-start(bf16[1024,256]{1,0:T(8,128)(2,1)S(1)} %copy-done.1), channel_id=1, source_target_pairs={{0,1},{1,0},{2,3},{3,2},{4,5},{5,4},{6,7},{7,6},{8,9},{9,8},{10,11... | collective-permute-start | bytes 1572872 | tf_op jit(solution)/shard_map/ppermute | solution.py:42
  24.1 8.1 %copy-start.3 = (f32[256]{0:T(256)S(1)}, f32[256]{0:T(256)}, u32[]{:S(2)}) copy-start(f32[256]{0:T(256)} %param.18) | copy-start | bytes 3076
  27.9 11.4 %all-to-all-start.1 = ((bf16[16,8,1024]{2,1,0:T(8,128)(2,1)}), bf16[16,8,1024]{2,1,0:T(8,128)(2,1)S(1)}, u32[]{:S(2)}, u32[]{:S(2)}) async-start(bf16[16,8,1024]{2,1,0:T(8,128)(2,1)} %attend.1), calls=%async_computation.1 | async-start | bytes 524288 | tf_op jit(solution)/shard_map/all_to_all | solution.py:448
  32.2 23.8 %collective-permute-start = (f32[17,256]{1,0:T(8,128)S(1)}, f32[17,256]{1,0:T(8,128)S(1)}, u32[]{:S(2)}, u32[]{:S(2)}) collective-permute-start(f32[17,256]{1,0:T(8,128)S(1)} %pad_maximum_fusion.2), channel_id=1, source_target_pairs={{0,1},{1,0},{2,3},{3,2},{4,5},{5,4},{6,7},{7,6},{8,9},{9,8},{10,11... | collective-permute-start | bytes 52232 | tf_op jit(solution)/shard_map/ppermute | solution.py:42
  40.5 16.1 %all-to-all-start.2 = ((bf16[8,16,512]{2,1,0:T(8,128)(2,1)}), bf16[8,16,512]{2,1,0:T(8,128)(2,1)S(1)}, u32[]{:S(2)}, u32[]{:S(2)}) async-start(bf16[8,16,512]{2,1,0:T(8,128)(2,1)} %pad_maximum_fusion.1), calls=%async_computation.2 | async-start | bytes 262144 | tf_op jit(solution)/shard_map/all_to_all | solution.py:460
  53.1 53.0 %collective-permute-start.7 = (bf16[512,1536]{1,0:T(8,128)(2,1)}, bf16[512,1536]{1,0:T(8,128)(2,1)S(1)}, u32[]{:S(2)}, u32[]{:S(2)}) collective-permute-start(bf16[512,1536]{1,0:T(8,128)(2,1)} %get-tuple-element.13), channel_id=1, source_target_pairs={{0,16},{8,24},{16,0},{24,8},{1,17},{9,25},{17,1},{25,9},{2,18},{10... | collective-permute-start | bytes 4718600 | tf_op jit(solution)/shard_map/ppermute | solution.py:42
  54.5 54.0 %collective-permute-start.8 = (bf16[512,1536]{1,0:T(8,128)(2,1)}, bf16[512,1536]{1,0:T(8,128)(2,1)S(1)}, u32[]{:S(2)}, u32[]{:S(2)}) collective-permute-start(bf16[512,1536]{1,0:T(8,128)(2,1)} %get-tuple-element.14), channel_id=1, source_target_pairs={{0,4},{2,6},{4,0},{6,2},{1,5},{3,7},{5,1},{7,3},{8,12},{10,14},{12... | collective-permute-start | bytes 4718600 | tf_op jit(solution)/shard_map/ppermute | solution.py:42
  57.4 20.0 %all-to-all-start.3 = ((bf16[16,16,512]{2,1,0:T(8,128)(2,1)}), bf16[16,16,512]{2,1,0:T(8,128)(2,1)S(1)}, u32[]{:S(2)}, u32[]{:S(2)}) async-start(bf16[16,16,512]{2,1,0:T(8,128)(2,1)} %broadcast_in_dim.54), calls=%async_computation.3 | async-start | bytes 524288 | tf_op jit(solution)/shard_map/all_to_all | solution.py:37
  65.8 23.2 %collective-permute-start.5 = (f32[1,512]{1,0:T(1,128)S(1)}, f32[1,512]{1,0:T(1,128)S(1)}, u32[]{:S(2)}, u32[]{:S(2)}) collective-permute-start(f32[1,512]{1,0:T(1,128)S(1)} %pad_maximum_fusion.4.gain), channel_id=1, source_target_pairs={{0,16},{8,24},{16,0},{24,8},{1,17},{9,25},{17,1},{25,9},{2,18},{10... | collective-permute-start | bytes 6152 | tf_op jit(solution)/shard_map/ppermute | solution.py:42
  67.7 22.7 %collective-permute-start.6 = (f32[1,512]{1,0:T(1,128)S(1)}, f32[1,512]{1,0:T(1,128)S(1)}, u32[]{:S(2)}, u32[]{:S(2)}) collective-permute-start(f32[1,512]{1,0:T(1,128)S(1)} %pad_maximum_fusion.4.gain), channel_id=1, source_target_pairs={{0,4},{2,6},{4,0},{6,2},{1,5},{3,7},{5,1},{7,3},{8,12},{10,14},{12... | collective-permute-start | bytes 6152 | tf_op jit(solution)/shard_map/ppermute | solution.py:42
  82.2 26.8 %collective-permute-start.10 = (bf16[4,136,384]{2,1,0:T(8,128)(2,1)S(1)}, bf16[4,136,384]{2,1,0:T(8,128)(2,1)S(1)}, u32[]{:S(2)}, u32[]{:S(2)}) collective-permute-start(bf16[4,136,384]{2,1,0:T(8,128)(2,1)S(1)} %get-tuple-element.17), channel_id=1, source_target_pairs={{0,24},{8,0},{16,8},{24,16},{1,25},{9,1},{17,9},{25,17},{2,26},{10... | collective-permute-start | bytes 1253384 | tf_op jit(solution)/shard_map/ppermute | solution.py:42
  89.1 20.0 %collective-permute-start.9 = (bf16[4,136,384]{2,1,0:T(8,128)(2,1)S(1)}, bf16[4,136,384]{2,1,0:T(8,128)(2,1)S(1)}, u32[]{:S(2)}, u32[]{:S(2)}) collective-permute-start(bf16[4,136,384]{2,1,0:T(8,128)(2,1)S(1)} %get-tuple-element.16), channel_id=1, source_target_pairs={{0,8},{8,16},{16,24},{24,0},{1,9},{9,17},{17,25},{25,1},{2,10},{10... | collective-permute-start | bytes 1253384 | tf_op jit(solution)/shard_map/ppermute | solution.py:42
  90.4 10.1 %collective-permute-start.3 = (bf16[4,2,2,8,512]{4,3,2,1,0:T(8,128)(2,1)S(1)}, bf16[4,2,2,8,512]{4,3,2,1,0:T(8,128)(2,1)S(1)}, u32[]{:S(2)}, u32[]{:S(2)}) collective-permute-start(bf16[4,2,2,8,512]{4,3,2,1,0:T(8,128)(2,1)S(1)} %bitcast.94), channel_id=1, source_target_pairs={{0,16},{8,24},{16,0},{24,8},{1,17},{9,25},{17,1},{25,9},{2,18},{10... | collective-permute-start | bytes 393224 | tf_op jit(solution)/shard_map/ppermute | solution.py:42
  100.4 5.3 %collective-permute-start.4 = (bf16[4,2,2,8,512]{4,3,2,1,0:T(8,128)(2,1)S(1)}, bf16[4,2,2,8,512]{4,3,2,1,0:T(8,128)(2,1)S(1)}, u32[]{:S(2)}, u32[]{:S(2)}) collective-permute-start(bf16[4,2,2,8,512]{4,3,2,1,0:T(8,128)(2,1)S(1)} %bitcast.93), channel_id=1, source_target_pairs={{0,4},{2,6},{4,0},{6,2},{1,5},{3,7},{5,1},{7,3},{8,12},{10,14},{12... | collective-permute-start | bytes 393224 | tf_op jit(solution)/shard_map/ppermute | solution.py:42
  105.8 9.5 %collective-permute-start.14 = (bf16[4,136,384]{2,1,0:T(8,128)(2,1)S(1)}, bf16[4,136,384]{2,1,0:T(8,128)(2,1)S(1)}, u32[]{:S(2)}, u32[]{:S(2)}) collective-permute-start(bf16[4,136,384]{2,1,0:T(8,128)(2,1)S(1)} %get-tuple-element.20), channel_id=1, source_target_pairs={{0,2},{2,4},{4,6},{6,0},{1,3},{3,5},{5,7},{7,1},{8,10},{10,12},{12... | collective-permute-start | bytes 1253384 | tf_op jit(solution)/shard_map/ppermute | solution.py:42
  106.1 9.2 %collective-permute-start.15 = (bf16[4,136,384]{2,1,0:T(8,128)(2,1)S(1)}, bf16[4,136,384]{2,1,0:T(8,128)(2,1)S(1)}, u32[]{:S(2)}, u32[]{:S(2)}) collective-permute-start(bf16[4,136,384]{2,1,0:T(8,128)(2,1)S(1)} %get-tuple-element.21), channel_id=1, source_target_pairs={{0,6},{2,0},{4,2},{6,4},{1,7},{3,1},{5,3},{7,5},{8,14},{10,8},{12,... | collective-permute-start | bytes 1253384 | tf_op jit(solution)/shard_map/ppermute | solution.py:42
  109.3 8.7 %collective-permute-start.11 = (bf16[136,384]{1,0:T(8,128)(2,1)S(1)}, bf16[136,384]{1,0:T(8,128)(2,1)S(1)}, u32[]{:S(2)}, u32[]{:S(2)}) collective-permute-start(bf16[136,384]{1,0:T(8,128)(2,1)S(1)} %get-tuple-element.26), channel_id=1, source_target_pairs={{0,2},{2,4},{4,6},{6,0},{1,3},{3,5},{5,7},{7,1},{8,10},{10,12},{12... | collective-permute-start | bytes 313352 | tf_op jit(solution)/shard_map/ppermute | solution.py:42
  109.4 9.8 %collective-permute-start.12 = (bf16[136,384]{1,0:T(8,128)(2,1)S(1)}, bf16[136,384]{1,0:T(8,128)(2,1)S(1)}, u32[]{:S(2)}, u32[]{:S(2)}) collective-permute-start(bf16[136,384]{1,0:T(8,128)(2,1)S(1)} %get-tuple-element.28), channel_id=1, source_target_pairs={{0,4},{2,6},{4,0},{6,2},{1,5},{3,7},{5,1},{7,3},{8,12},{10,14},{12... | collective-permute-start | bytes 313352 | tf_op jit(solution)/shard_map/ppermute | solution.py:42
  110.6 8.6 %collective-permute-start.13 = (bf16[136,384]{1,0:T(8,128)(2,1)S(1)}, bf16[136,384]{1,0:T(8,128)(2,1)S(1)}, u32[]{:S(2)}, u32[]{:S(2)}) collective-permute-start(bf16[136,384]{1,0:T(8,128)(2,1)S(1)} %get-tuple-element.27), channel_id=1, source_target_pairs={{0,6},{2,0},{4,2},{6,4},{1,7},{3,1},{5,3},{7,5},{8,14},{10,8},{12,... | collective-permute-start | bytes 313352 | tf_op jit(solution)/shard_map/ppermute | solution.py:42
  115.5 6.2 %collective-permute-start.16 = (bf16[136,384]{1,0:T(8,128)(2,1)S(1)}, bf16[136,384]{1,0:T(8,128)(2,1)S(1)}, u32[]{:S(2)}, u32[]{:S(2)}) collective-permute-start(bf16[136,384]{1,0:T(8,128)(2,1)S(1)} %get-tuple-element.29), channel_id=1, source_target_pairs={{0,8},{8,16},{16,24},{24,0},{1,9},{9,17},{17,25},{25,1},{2,10},{10... | collective-permute-start | bytes 313352 | tf_op jit(solution)/shard_map/ppermute | solution.py:42
  115.6 6.1 %collective-permute-start.17 = (bf16[136,384]{1,0:T(8,128)(2,1)S(1)}, bf16[136,384]{1,0:T(8,128)(2,1)S(1)}, u32[]{:S(2)}, u32[]{:S(2)}) collective-permute-start(bf16[136,384]{1,0:T(8,128)(2,1)S(1)} %get-tuple-element.31), channel_id=1, source_target_pairs={{0,16},{8,24},{16,0},{24,8},{1,17},{9,25},{17,1},{25,9},{2,18},{10... | collective-permute-start | bytes 313352 | tf_op jit(solution)/shard_map/ppermute | solution.py:42
  118.0 4.3 %collective-permute-start.18 = (bf16[136,384]{1,0:T(8,128)(2,1)S(1)}, bf16[136,384]{1,0:T(8,128)(2,1)S(1)}, u32[]{:S(2)}, u32[]{:S(2)}) collective-permute-start(bf16[136,384]{1,0:T(8,128)(2,1)S(1)} %get-tuple-element.30), channel_id=1, source_target_pairs={{0,24},{8,0},{16,8},{24,16},{1,25},{9,1},{17,9},{25,17},{2,26},{10... | collective-permute-start | bytes 313352 | tf_op jit(solution)/shard_map/ppermute | solution.py:42
  122.6 36.0 %copy-start = (f32[256,384]{1,0:T(8,128)}, f32[256,384]{1,0:T(8,128)S(1)}, u32[]{:S(2)}) copy-start(f32[256,384]{1,0:T(8,128)S(1)} %get-tuple-element.25) | copy-start | bytes 1179652
where the time goes:
time: 159 us
  waiting for transfers between devices  53 us (33%)
  starting transfers between devices  48.5 us (31%)
  blocking collectives  34.9 us (22%)
  Pallas kernels  15.8 us (10%)
  other arithmetic  3.9 us (2%)
    all_to_all x2, blocking collectives, sent_to_all(): lax.all_to_all(jnp.broadcast_to(x[None], (length, *x.shape)), axis, 0, 0,...  34.9 us
    ppermute x19, waiting for transfers between devices, shifted(): lax.ppermute(x, axis, [(k, (k + by) % length) for k in range(length)])  26.4 us
    ppermute x19, starting transfers between devices, shifted(): lax.ppermute(x, axis, [(k, (k + by) % length) for k in range(length)])  22.8 us
    all_to_all x1, waiting for transfers between devices, local(): parts = lax.all_to_all(parts, MP, split_axis=0, concat_axis=0, tiled=True)  11.3 us
    all_to_all x1, starting transfers between devices, sent_to_all(): lax.all_to_all(jnp.broadcast_to(x[None], (length, *x.shape)), axis, 0, 0,...  8.44 us
    all_to_all x1, starting transfers between devices, local(): lax.all_to_all(partial_out.reshape(batches, per_batch * seq_count, -1), '...  8.19 us
    all_to_all x1, waiting for transfers between devices, sent_to_all(): lax.all_to_all(jnp.broadcast_to(x[None], (length, *x.shape)), axis, 0, 0,...  7.92 us
    all_to_all x1, waiting for transfers between devices, local(): mine = lax.all_to_all(attended, XY, 0, 0, tiled=True)  6.9 us
  transfers between devices with their start and end apart: 23, of which 11 were waited for; matrix products, arithmetic and copies ran while one was open for 3% of the time, Pallas kernels for 10%

commit v1 on v0

--- a/solution.py
+++ b/solution.py
@@ -434,6 +434,14 @@
     far_head_weight = shifted(head_weight, "mp_2", 1)
     far_out_weight = shifted(out_weight, "mp_2", 1)
 
+    both_out = jnp.concatenate(
+        [
+            jnp.where(first_core, out_weight, far_out_weight),
+            jnp.where(first_core, far_out_weight, out_weight),
+        ],
+        axis=1,
+    )
+    both_out = lax.optimization_barrier(both_out)
     parts = query_parts(stream, input_gain, query_weight).reshape(members, seq_count, -1)
     parts = lax.all_to_all(parts, MP, split_axis=0, concat_axis=0, tiled=True)
     owners = token_owners(page_table, lengths, *page_cache.shape[2:4])
@@ -451,11 +459,7 @@
     weight_x = shifted(weight_x, "mp_0", side // 2)
     weight_y = shifted(weight_y, "mp_1", side // 2)
     mine = mine.reshape(side * side * seq_count, -1)
-    near_out = jnp.dot(mine, out_weight, preferred_element_type=jnp.float32)
-    far_out = jnp.dot(mine, far_out_weight, preferred_element_type=jnp.float32)
-    partial_out = jnp.concatenate(
-        [jnp.where(first_core, near_out, far_out), jnp.where(first_core, far_out, near_out)], axis=1
-    ).astype(jnp.bfloat16)
+    partial_out = jnp.dot(mine, both_out, preferred_element_type=jnp.float32).astype(jnp.bfloat16)
     per_batch = side * side // batches
     arrived = lax.all_to_all(
         partial_out.reshape(batches, per_batch * seq_count, -1),

time: 159 us -> 161 us (1.013)
  no operation moved by 1% of the time
where the time goes in v1:
time: 161 us; the launch traced here: 160 us
  waiting for transfers between devices  54.1 us (34%)
  starting transfers between devices  48.5 us (30%)
  blocking collectives  34.9 us (22%)
  Pallas kernels  15.9 us (10%)
  other arithmetic  4.12 us (3%)
    all_to_all x2, blocking collectives, sent_to_all(): lax.all_to_all(jnp.broadcast_to(x[None], (length, *x.shape)), axis, 0, 0,...  34.9 us
    ppermute x19, waiting for transfers between devices, shifted(): lax.ppermute(x, axis, [(k, (k + by) % length) for k in range(length)])  26.3 us
    ppermute x19, starting transfers between devices, shifted(): lax.ppermute(x, axis, [(k, (k + by) % length) for k in range(length)])  22.8 us
    all_to_all x1, waiting for transfers between devices, local(): parts = lax.all_to_all(parts, MP, split_axis=0, concat_axis=0, tiled=True)  11.5 us
    all_to_all x1, starting transfers between devices, sent_to_all(): lax.all_to_all(jnp.broadcast_to(x[None], (length, *x.shape)), axis, 0, 0,...  8.45 us
    all_to_all x1, starting transfers between devices, local(): lax.all_to_all(partial_out.reshape(batches, per_batch * seq_count, -1), '...  8.18 us
    all_to_all x1, waiting for transfers between devices, sent_to_all(): lax.all_to_all(jnp.broadcast_to(x[None], (length, *x.shape)), axis, 0, 0,...  7.92 us
    all_to_all x1, waiting for transfers between devices, local(): mine = lax.all_to_all(attended, XY, 0, 0, tiled=True)  7.69 us
  transfers between devices with their start and end apart: 23, of which 11 were waited for; matrix products, arithmetic and copies ran while one was open for 3% of the time, Pallas kernels for 10%

profile of v1, /device:TPU:1, one launch (start us, length us, event | category | flops | bytes accessed | tf_op | source)
XLA Modules:
  0.0 160.4 jit_solution(13361975092234063248)
XLA Ops:
  0.7 3.3 %collective-permute-start.2 = (bf16[256,12288]{1,0:T(8,128)(2,1)}, bf16[256,12288]{1,0:T(8,128)(2,1)}, u32[]{:S(2)}, u32[]{:S(2)}) collective-permute-start(bf16[256,12288]{1,0:T(8,128)(2,1)} %near_weight.3), channel_id=1, source_target_pairs={{0,1},{1,0},{2,3},{3,2},{4,5},{5,4},{6,7},{7,6},{8,9},{9,8},{10,11... | collective-permute-start | bytes 18874376 | tf_op jit(solution)/shard_map/ppermute | solution.py:42
  3.9 0.7 bitcast_convert_fusion.1
  4.7 0.7 pad_maximum_fusion.2
  5.3 0.0 collective-permute-start
  5.4 0.5 collective-permute-start.1
  5.9 2.3 %query_parts.1 = bf16[256,1152]{1,0:T(8,128)(2,1)} custom-call(bf16[256,256]{1,0:T(8,128)(2,1)} %stream.1, f32[1,256]{1,0:T(1,128)} %bitcast.93, bf16[256,1024]{1,0:T(8,128)(2,1)} %weight.1), custom_call_target="tpu_custom_call" | custom-call | tf_op jit(solution)/shard_map/query_parts/pallas_call | solution.py:60
  8.1 5.5 %all-to-all-start = ((bf16[32,8,1152]{2,1,0:T(8,128)(2,1)}), bf16[32,8,1152]{2,1,0:T(8,128)(2,1)S(1)}, u32[]{:S(2)}, u32[]{:S(2)}) async-start(bf16[32,8,1152]{2,1,0:T(8,128)(2,1)} %bitcast.8), calls=%async_computation | async-start | bytes 1179648 | tf_op jit(solution)/shard_map/all_to_all | solution.py:446
  13.7 0.1 broadcast_subtract_fusion
  13.8 0.1 multiply_sine_fusion
  13.9 0.1 iota_compare_fusion.2
  13.9 0.1 pad_add_fusion.place
  14.0 0.1 concatenate.21.table
  14.1 0.2 select_reduce_fusion.1
  14.3 0.1 fusion.14
  14.4 11.5 %all-to-all-done = bf16[32,8,1152]{2,1,0:T(8,128)(2,1)S(1)} async-done(((bf16[32,8,1152]{2,1,0:T(8,128)(2,1)}), bf16[32,8,1152]{2,1,0:T(8,128)(2,1)S(1)}, u32[]{:S(2)}, u32[]{:S(2)}) %all-to-all-start) | async-done | bytes 589856 | tf_op jit(solution)/shard_map/all_to_all | solution.py:446
  25.9 0.1 convert_reduce_fusion.sums
  26.0 3.9 %attend.1 = bf16[16,8,1024]{2,1,0:T(8,128)(2,1)} custom-call(f32[8,1152]{1,0:T(8,128)S(1)} %convert_reduce_fusion.sums, f32[8,1280]{1,0:T(8,128)S(1)} %concatenate.21.table, s32[1,8192]{1,0:T(1,128)S(1)} %bitcast.82, bf16[2,1,64,128,128]{4,3,2,1,0:T(8,128)(2,1)} %pages.1), custom_call_target="tpu_custom_call" | custom-call | tf_op jit(solution)/shard_map/attend/pallas_call | solution.py:167
  29.9 3.5 %all-to-all-start.1 = ((bf16[16,8,1024]{2,1,0:T(8,128)(2,1)}), bf16[16,8,1024]{2,1,0:T(8,128)(2,1)S(1)}, u32[]{:S(2)}, u32[]{:S(2)}) async-start(bf16[16,8,1024]{2,1,0:T(8,128)(2,1)} %attend.1), calls=%async_computation.1 | async-start | bytes 524288 | tf_op jit(solution)/shard_map/all_to_all | solution.py:456
  33.4 0.1 broadcast_select_fusion.1
  33.5 0.1 pad_maximum_fusion
  33.6 7.7 %all-to-all-done.1 = bf16[16,8,1024]{2,1,0:T(8,128)(2,1)S(1)} async-done(((bf16[16,8,1024]{2,1,0:T(8,128)(2,1)}), bf16[16,8,1024]{2,1,0:T(8,128)(2,1)S(1)}, u32[]{:S(2)}, u32[]{:S(2)}) %all-to-all-start.1) | async-done | bytes 262176 | tf_op jit(solution)/shard_map/all_to_all | solution.py:456
  41.3 1.0 convolution_convert_fusion
  42.3 8.2 %all-to-all-start.2 = ((bf16[8,16,512]{2,1,0:T(8,128)(2,1)}), bf16[8,16,512]{2,1,0:T(8,128)(2,1)S(1)}, u32[]{:S(2)}, u32[]{:S(2)}) async-start(bf16[8,16,512]{2,1,0:T(8,128)(2,1)} %bitcast.11), calls=%async_computation.2 | async-start | bytes 262144 | tf_op jit(solution)/shard_map/all_to_all | solution.py:464
  50.5 4.4 %partner_weights.1 = (bf16[512,1536]{1,0:T(8,128)(2,1)}, bf16[512,1536]{1,0:T(8,128)(2,1)}) custom-call(s32[3]{0:T(128)S(1)} %pad_add_fusion.place, bf16[256,12288]{1,0:T(8,128)(2,1)} %near_weight.3, bf16[256,12288]{1,0:T(8,128)(2,1)} %collective-permute-done.2.far_weight), custom_call_target="tpu_custom_call" | custom-call | tf_op jit(solution)/shard_map/partner_weights/pallas_call | solution.py:330
  54.8 1.4 collective-permute-start.7
  56.2 1.5 collective-permute-start.8
  57.8 0.6 all-to-all-done.2
  58.4 0.7 broadcast_in_dim.54
  59.1 8.4 %all-to-all-start.3 = ((bf16[16,16,512]{2,1,0:T(8,128)(2,1)}), bf16[16,16,512]{2,1,0:T(8,128)(2,1)S(1)}, u32[]{:S(2)}, u32[]{:S(2)}) async-start(bf16[16,16,512]{2,1,0:T(8,128)(2,1)} %broadcast_in_dim.54), calls=%async_computation.3 | async-start | bytes 524288 | tf_op jit(solution)/shard_map/all_to_all | solution.py:37
  67.6 1.9 %collective-permute-start.5 = (f32[1,512]{1,0:T(1,128)S(1)}, f32[1,512]{1,0:T(1,128)S(1)}, u32[]{:S(2)}, u32[]{:S(2)}) collective-permute-start(f32[1,512]{1,0:T(1,128)S(1)} %pad_maximum_fusion.4.gain), channel_id=1, source_target_pairs={{0,16},{8,24},{16,0},{24,8},{1,17},{9,25},{17,1},{25,9},{2,18},{10... | collective-permute-start | bytes 6152 | tf_op jit(solution)/shard_map/ppermute | solution.py:42
  69.5 1.8 %collective-permute-start.6 = (f32[1,512]{1,0:T(1,128)S(1)}, f32[1,512]{1,0:T(1,128)S(1)}, u32[]{:S(2)}, u32[]{:S(2)}) collective-permute-start(f32[1,512]{1,0:T(1,128)S(1)} %pad_maximum_fusion.4.gain), channel_id=1, source_target_pairs={{0,4},{2,6},{4,0},{6,2},{1,5},{3,7},{5,1},{7,3},{8,12},{10,14},{12... | collective-permute-start | bytes 6152 | tf_op jit(solution)/shard_map/ppermute | solution.py:42
  71.3 7.9 %all-to-all-done.3 = bf16[16,16,512]{2,1,0:T(8,128)(2,1)S(1)} async-done(((bf16[16,16,512]{2,1,0:T(8,128)(2,1)}), bf16[16,16,512]{2,1,0:T(8,128)(2,1)S(1)}, u32[]{:S(2)}, u32[]{:S(2)}) %all-to-all-start.3) | async-done | bytes 262176 | tf_op jit(solution)/shard_map/all_to_all | solution.py:37
  79.2 4.8 %head_partials.1 = (bf16[4,136,384]{2,1,0:T(8,128)(2,1)S(1)}, bf16[4,136,384]{2,1,0:T(8,128)(2,1)S(1)}, bf16[4,136,384]{2,1,0:T(8,128)(2,1)S(1)}, bf16[4,136,384...) custom-call(s32[3]{0:T(128)S(1)} %pad_add_fusion.place, ...), custom_call_target="tpu_custom_call" | custom-call | tf_op jit(solution)/shard_map/head_partials/pallas_call | solution.py:266
  84.0 1.5 collective-permute-start.10
  85.5 5.4 %collective-permute-done.5.gain_x = f32[1,512]{1,0:T(1,128)S(1)} collective-permute-done((f32[1,512]{1,0:T(1,128)S(1)}, f32[1,512]{1,0:T(1,128)S(1)}, u32[]{:S(2)}, u32[]{:S(2)}) %collective-permute-start.5) | collective-permute-done | bytes 2080 | tf_op jit(solution)/shard_map/ppermute | solution.py:42
  90.8 0.0 collective-permute-start.9
  90.9 1.2 collective-permute-done.6.gain_y
  92.2 1.8 %collective-permute-start.3 = (bf16[4,2,2,8,512]{4,3,2,1,0:T(8,128)(2,1)S(1)}, bf16[4,2,2,8,512]{4,3,2,1,0:T(8,128)(2,1)S(1)}, u32[]{:S(2)}, u32[]{:S(2)}) collective-permute-start(bf16[4,2,2,8,512]{4,3,2,1,0:T(8,128)(2,1)S(1)} %bitcast.86), channel_id=1, source_target_pairs={{0,16},{8,24},{16,0},{24,8},{1,17},{9,25},{17,1},{25,9},{2,18},{10... | collective-permute-start | bytes 393224 | tf_op jit(solution)/shard_map/ppermute | solution.py:42
  94.0 8.3 %collective-permute-done.3.rows_x = bf16[4,2,2,8,512]{4,3,2,1,0:T(8,128)(2,1)S(1)} collective-permute-done((bf16[4,2,2,8,512]{4,3,2,1,0:T(8,128)(2,1)S(1)}, bf16[4,2,2,8,512]{4,3,2,1,0:T(8,128)(2,1)S(1)}, u32[]{:S(2)}, u32[]{:S(2)}) %collective-permute-start.3) | collective-permute-done | bytes 131104 | tf_op jit(solution)/shard_map/ppermute | solution.py:42
  102.2 5.3 %collective-permute-done.4.rows_y = bf16[4,2,2,8,512]{4,3,2,1,0:T(8,128)(2,1)S(1)} collective-permute-done((bf16[4,2,2,8,512]{4,3,2,1,0:T(8,128)(2,1)S(1)}, bf16[4,2,2,8,512]{4,3,2,1,0:T(8,128)(2,1)S(1)}, u32[]{:S(2)}, u32[]{:S(2)}) %collective-permute-start.4) | collective-permute-done | bytes 131104 | tf_op jit(solution)/shard_map/ppermute | solution.py:42
  107.5 0.3 collective-permute-start.14
  107.9 2.3 %collective-permute-start.15 = (bf16[4,136,384]{2,1,0:T(8,128)(2,1)S(1)}, bf16[4,136,384]{2,1,0:T(8,128)(2,1)S(1)}, u32[]{:S(2)}, u32[]{:S(2)}) collective-permute-start(bf16[4,136,384]{2,1,0:T(8,128)(2,1)S(1)} %get-tuple-element.21), channel_id=1, source_target_pairs={{0,6},{2,0},{4,2},{6,4},{1,7},{3,1},{5,3},{7,5},{8,14},{10,8},{12,... | collective-permute-start | bytes 1253384 | tf_op jit(solution)/shard_map/ppermute | solution.py:42
  110.2 0.6 head_partner.1
  110.9 0.2 add_convert_fusion.1
  111.1 0.1 collective-permute-start.11
  111.2 1.2 collective-permute-start.12
  112.4 1.5 collective-permute-start.13
  113.9 3.1 %collective-permute-done.14 = bf16[4,136,384]{2,1,0:T(8,128)(2,1)S(1)} collective-permute-done((bf16[4,136,384]{2,1,0:T(8,128)(2,1)S(1)}, bf16[4,136,384]{2,1,0:T(8,128)(2,1)S(1)}, u32[]{:S(2)}, u32[]{:S(2)}) %collective-permute-start.14) | collective-permute-done | bytes 417824 | tf_op jit(solution)/shard_map/ppermute | solution.py:42
  117.1 0.2 add_convert_fusion
  117.3 0.1 collective-permute-start.16
  117.4 2.4 %collective-permute-start.17 = (bf16[136,384]{1,0:T(8,128)(2,1)S(1)}, bf16[136,384]{1,0:T(8,128)(2,1)S(1)}, u32[]{:S(2)}, u32[]{:S(2)}) collective-permute-start(bf16[136,384]{1,0:T(8,128)(2,1)S(1)} %get-tuple-element.33), channel_id=1, source_target_pairs={{0,16},{8,24},{16,0},{24,8},{1,17},{9,25},{17,1},{25,9},{2,18},{10... | collective-permute-start | bytes 313352 | tf_op jit(solution)/shard_map/ppermute | solution.py:42
  119.8 1.1 collective-permute-start.18
  121.0 0.1 fusion.4
  121.1 0.1 slice_multiply_fusion.1
  121.1 2.4 %collective-permute-done.16 = bf16[136,384]{1,0:T(8,128)(2,1)S(1)} collective-permute-done((bf16[136,384]{1,0:T(8,128)(2,1)S(1)}, bf16[136,384]{1,0:T(8,128)(2,1)S(1)}, u32[]{:S(2)}, u32[]{:S(2)}) %collective-permute-start.16) | collective-permute-done | bytes 104480 | tf_op jit(solution)/shard_map/ppermute | solution.py:42
  123.6 0.6 collective-permute-done.18
  124.1 0.1 fusion.2
  124.2 0.1 slice_multiply_fusion
  124.3 0.1 fusion.23
  124.4 0.2 exponential_reduce_fusion
  124.7 22.1 %all_to_all.30 = f32[32,2,256]{2,1,0:T(2,128)S(1)} all-to-all(f32[32,2,256]{2,1,0:T(2,128)S(1)} %broadcast_in_dim.55), channel_id=1, replica_groups=mesh['batch'=8,'mp_0'=4,'mp_1'=4,'mp_2'=2] {'mp_0','mp_1','mp_2'}, dimensions={0} | all-to-all | bytes 131072 | tf_op jit(solution)/shard_map/all_to_all | solution.py:37
  146.8 0.1 slice_reduce_fusion.1
  146.9 12.8 %all_to_all.31 = f32[8,2,256]{2,1,0:T(2,128)S(1)} all-to-all(f32[8,2,256]{2,1,0:T(2,128)S(1)} %broadcast_in_dim.56), channel_id=1, replica_groups=mesh['batch'=8,'mp_0'=4,'mp_1'=4,'mp_2'=2] {'batch'}, dimensions={0} | all-to-all | bytes 32768 | tf_op jit(solution)/shard_map/all_to_all | solution.py:37
  159.8 0.6 log_add_fusion
  (45 shorter events, 0.4 us)
Async XLA Ops:
  0.6 13.0 %copy-start.5 = (s32[8]{0:T(128)S(1)}, s32[8]{0:T(128)}, u32[]{:S(2)}) copy-start(s32[8]{0:T(128)} %param.17) | copy-start | bytes 100
  0.6 13.4 %copy-start.2 = (f32[1024]{0:T(1024)S(1)}, f32[1024]{0:T(1024)}, u32[]{:S(2)}) copy-start(f32[1024]{0:T(1024)} %param.12) | copy-start | bytes 12292
  0.7 13.4 %copy-start.4 = (s32[8,24]{1,0:T(8,128)S(1)}, s32[8,24]{1,0:T(8,128)}, u32[]{:S(2)}) copy-start(s32[8,24]{1,0:T(8,128)} %param.16) | copy-start | bytes 2308
  0.7 49.8 %collective-permute-start.2 = (bf16[256,12288]{1,0:T(8,128)(2,1)}, bf16[256,12288]{1,0:T(8,128)(2,1)}, u32[]{:S(2)}, u32[]{:S(2)}) collective-permute-start(bf16[256,12288]{1,0:T(8,128)(2,1)} %near_weight.3), channel_id=1, source_target_pairs={{0,1},{1,0},{2,3},{3,2},{4,5},{5,4},{6,7},{7,6},{8,9},{9,8},{10,11... | collective-permute-start | bytes 18874376 | tf_op jit(solution)/shard_map/ppermute | solution.py:42
  5.3 52.4 %collective-permute-start = (f32[17,256]{1,0:T(8,128)S(1)}, f32[17,256]{1,0:T(8,128)S(1)}, u32[]{:S(2)}, u32[]{:S(2)}) collective-permute-start(f32[17,256]{1,0:T(8,128)S(1)} %pad_maximum_fusion.2), channel_id=1, source_target_pairs={{0,1},{1,0},{2,3},{3,2},{4,5},{5,4},{6,7},{7,6},{8,9},{9,8},{10,11... | collective-permute-start | bytes 52232 | tf_op jit(solution)/shard_map/ppermute | solution.py:42
  5.4 28.0 %collective-permute-start.1 = (bf16[1024,256]{1,0:T(8,128)(2,1)}, bf16[1024,256]{1,0:T(8,128)(2,1)S(1)}, u32[]{:S(2)}, u32[]{:S(2)}) collective-permute-start(bf16[1024,256]{1,0:T(8,128)(2,1)} %param.14), channel_id=1, source_target_pairs={{0,1},{1,0},{2,3},{3,2},{4,5},{5,4},{6,7},{7,6},{8,9},{9,8},{10,11... | collective-permute-start | bytes 1572872 | tf_op jit(solution)/shard_map/ppermute | solution.py:42
  8.1 17.8 %all-to-all-start = ((bf16[32,8,1152]{2,1,0:T(8,128)(2,1)}), bf16[32,8,1152]{2,1,0:T(8,128)(2,1)S(1)}, u32[]{:S(2)}, u32[]{:S(2)}) async-start(bf16[32,8,1152]{2,1,0:T(8,128)(2,1)} %bitcast.8), calls=%async_computation | async-start | bytes 1179648 | tf_op jit(solution)/shard_map/all_to_all | solution.py:446
  26.0 7.5 %copy-start.1 = (bf16[1024,256]{1,0:T(8,128)(2,1)S(1)}, bf16[1024,256]{1,0:T(8,128)(2,1)}, u32[]{:S(2)}) copy-start(bf16[1024,256]{1,0:T(8,128)(2,1)} %param.14) | copy-start | bytes 1572868
  29.9 11.4 %all-to-all-start.1 = ((bf16[16,8,1024]{2,1,0:T(8,128)(2,1)}), bf16[16,8,1024]{2,1,0:T(8,128)(2,1)S(1)}, u32[]{:S(2)}, u32[]{:S(2)}) async-start(bf16[16,8,1024]{2,1,0:T(8,128)(2,1)} %attend.1), calls=%async_computation.1 | async-start | bytes 524288 | tf_op jit(solution)/shard_map/all_to_all | solution.py:456
  42.3 16.1 %all-to-all-start.2 = ((bf16[8,16,512]{2,1,0:T(8,128)(2,1)}), bf16[8,16,512]{2,1,0:T(8,128)(2,1)S(1)}, u32[]{:S(2)}, u32[]{:S(2)}) async-start(bf16[8,16,512]{2,1,0:T(8,128)(2,1)} %bitcast.11), calls=%async_computation.2 | async-start | bytes 262144 | tf_op jit(solution)/shard_map/all_to_all | solution.py:464
  50.4 7.3 %copy-start.3 = (f32[256]{0:T(256)S(1)}, f32[256]{0:T(256)}, u32[]{:S(2)}) copy-start(f32[256]{0:T(256)} %param.18) | copy-start | bytes 3076
  54.8 53.0 %collective-permute-start.7 = (bf16[512,1536]{1,0:T(8,128)(2,1)}, bf16[512,1536]{1,0:T(8,128)(2,1)S(1)}, u32[]{:S(2)}, u32[]{:S(2)}) collective-permute-start(bf16[512,1536]{1,0:T(8,128)(2,1)} %get-tuple-element.13), channel_id=1, source_target_pairs={{0,16},{8,24},{16,0},{24,8},{1,17},{9,25},{17,1},{25,9},{2,18},{10... | collective-permute-start | bytes 4718600 | tf_op jit(solution)/shard_map/ppermute | solution.py:42
  56.2 54.0 %collective-permute-start.8 = (bf16[512,1536]{1,0:T(8,128)(2,1)}, bf16[512,1536]{1,0:T(8,128)(2,1)S(1)}, u32[]{:S(2)}, u32[]{:S(2)}) collective-permute-start(bf16[512,1536]{1,0:T(8,128)(2,1)} %get-tuple-element.14), channel_id=1, source_target_pairs={{0,4},{2,6},{4,0},{6,2},{1,5},{3,7},{5,1},{7,3},{8,12},{10,14},{12... | collective-permute-start | bytes 4718600 | tf_op jit(solution)/shard_map/ppermute | solution.py:42
  59.1 20.0 %all-to-all-start.3 = ((bf16[16,16,512]{2,1,0:T(8,128)(2,1)}), bf16[16,16,512]{2,1,0:T(8,128)(2,1)S(1)}, u32[]{:S(2)}, u32[]{:S(2)}) async-start(bf16[16,16,512]{2,1,0:T(8,128)(2,1)} %broadcast_in_dim.54), calls=%async_computation.3 | async-start | bytes 524288 | tf_op jit(solution)/shard_map/all_to_all | solution.py:37
  67.6 23.2 %collective-permute-start.5 = (f32[1,512]{1,0:T(1,128)S(1)}, f32[1,512]{1,0:T(1,128)S(1)}, u32[]{:S(2)}, u32[]{:S(2)}) collective-permute-start(f32[1,512]{1,0:T(1,128)S(1)} %pad_maximum_fusion.4.gain), channel_id=1, source_target_pairs={{0,16},{8,24},{16,0},{24,8},{1,17},{9,25},{17,1},{25,9},{2,18},{10... | collective-permute-start | bytes 6152 | tf_op jit(solution)/shard_map/ppermute | solution.py:42
  69.5 22.7 %collective-permute-start.6 = (f32[1,512]{1,0:T(1,128)S(1)}, f32[1,512]{1,0:T(1,128)S(1)}, u32[]{:S(2)}, u32[]{:S(2)}) collective-permute-start(f32[1,512]{1,0:T(1,128)S(1)} %pad_maximum_fusion.4.gain), channel_id=1, source_target_pairs={{0,4},{2,6},{4,0},{6,2},{1,5},{3,7},{5,1},{7,3},{8,12},{10,14},{12... | collective-permute-start | bytes 6152 | tf_op jit(solution)/shard_map/ppermute | solution.py:42
  84.0 26.9 %collective-permute-start.10 = (bf16[4,136,384]{2,1,0:T(8,128)(2,1)S(1)}, bf16[4,136,384]{2,1,0:T(8,128)(2,1)S(1)}, u32[]{:S(2)}, u32[]{:S(2)}) collective-permute-start(bf16[4,136,384]{2,1,0:T(8,128)(2,1)S(1)} %get-tuple-element.17), channel_id=1, source_target_pairs={{0,24},{8,0},{16,8},{24,16},{1,25},{9,1},{17,9},{25,17},{2,26},{10... | collective-permute-start | bytes 1253384 | tf_op jit(solution)/shard_map/ppermute | solution.py:42
  90.8 20.0 %collective-permute-start.9 = (bf16[4,136,384]{2,1,0:T(8,128)(2,1)S(1)}, bf16[4,136,384]{2,1,0:T(8,128)(2,1)S(1)}, u32[]{:S(2)}, u32[]{:S(2)}) collective-permute-start(bf16[4,136,384]{2,1,0:T(8,128)(2,1)S(1)} %get-tuple-element.16), channel_id=1, source_target_pairs={{0,8},{8,16},{16,24},{24,0},{1,9},{9,17},{17,25},{25,1},{2,10},{10... | collective-permute-start | bytes 1253384 | tf_op jit(solution)/shard_map/ppermute | solution.py:42
  92.2 10.1 %collective-permute-start.3 = (bf16[4,2,2,8,512]{4,3,2,1,0:T(8,128)(2,1)S(1)}, bf16[4,2,2,8,512]{4,3,2,1,0:T(8,128)(2,1)S(1)}, u32[]{:S(2)}, u32[]{:S(2)}) collective-permute-start(bf16[4,2,2,8,512]{4,3,2,1,0:T(8,128)(2,1)S(1)} %bitcast.86), channel_id=1, source_target_pairs={{0,16},{8,24},{16,0},{24,8},{1,17},{9,25},{17,1},{25,9},{2,18},{10... | collective-permute-start | bytes 393224 | tf_op jit(solution)/shard_map/ppermute | solution.py:42
  102.2 5.3 %collective-permute-start.4 = (bf16[4,2,2,8,512]{4,3,2,1,0:T(8,128)(2,1)S(1)}, bf16[4,2,2,8,512]{4,3,2,1,0:T(8,128)(2,1)S(1)}, u32[]{:S(2)}, u32[]{:S(2)}) collective-permute-start(bf16[4,2,2,8,512]{4,3,2,1,0:T(8,128)(2,1)S(1)} %bitcast.85), channel_id=1, source_target_pairs={{0,4},{2,6},{4,0},{6,2},{1,5},{3,7},{5,1},{7,3},{8,12},{10,14},{12... | collective-permute-start | bytes 393224 | tf_op jit(solution)/shard_map/ppermute | solution.py:42
  107.5 9.5 %collective-permute-start.14 = (bf16[4,136,384]{2,1,0:T(8,128)(2,1)S(1)}, bf16[4,136,384]{2,1,0:T(8,128)(2,1)S(1)}, u32[]{:S(2)}, u32[]{:S(2)}) collective-permute-start(bf16[4,136,384]{2,1,0:T(8,128)(2,1)S(1)} %get-tuple-element.20), channel_id=1, source_target_pairs={{0,2},{2,4},{4,6},{6,0},{1,3},{3,5},{5,7},{7,1},{8,10},{10,12},{12... | collective-permute-start | bytes 1253384 | tf_op jit(solution)/shard_map/ppermute | solution.py:42
  107.9 9.2 %collective-permute-start.15 = (bf16[4,136,384]{2,1,0:T(8,128)(2,1)S(1)}, bf16[4,136,384]{2,1,0:T(8,128)(2,1)S(1)}, u32[]{:S(2)}, u32[]{:S(2)}) collective-permute-start(bf16[4,136,384]{2,1,0:T(8,128)(2,1)S(1)} %get-tuple-element.21), channel_id=1, source_target_pairs={{0,6},{2,0},{4,2},{6,4},{1,7},{3,1},{5,3},{7,5},{8,14},{10,8},{12,... | collective-permute-start | bytes 1253384 | tf_op jit(solution)/shard_map/ppermute | solution.py:42
  111.1 8.7 %collective-permute-start.11 = (bf16[136,384]{1,0:T(8,128)(2,1)S(1)}, bf16[136,384]{1,0:T(8,128)(2,1)S(1)}, u32[]{:S(2)}, u32[]{:S(2)}) collective-permute-start(bf16[136,384]{1,0:T(8,128)(2,1)S(1)} %get-tuple-element.28), channel_id=1, source_target_pairs={{0,2},{2,4},{4,6},{6,0},{1,3},{3,5},{5,7},{7,1},{8,10},{10,12},{12... | collective-permute-start | bytes 313352 | tf_op jit(solution)/shard_map/ppermute | solution.py:42
  111.2 9.7 %collective-permute-start.12 = (bf16[136,384]{1,0:T(8,128)(2,1)S(1)}, bf16[136,384]{1,0:T(8,128)(2,1)S(1)}, u32[]{:S(2)}, u32[]{:S(2)}) collective-permute-start(bf16[136,384]{1,0:T(8,128)(2,1)S(1)} %get-tuple-element.30), channel_id=1, source_target_pairs={{0,4},{2,6},{4,0},{6,2},{1,5},{3,7},{5,1},{7,3},{8,12},{10,14},{12... | collective-permute-start | bytes 313352 | tf_op jit(solution)/shard_map/ppermute | solution.py:42
  112.4 8.6 %collective-permute-start.13 = (bf16[136,384]{1,0:T(8,128)(2,1)S(1)}, bf16[136,384]{1,0:T(8,128)(2,1)S(1)}, u32[]{:S(2)}, u32[]{:S(2)}) collective-permute-start(bf16[136,384]{1,0:T(8,128)(2,1)S(1)} %get-tuple-element.29), channel_id=1, source_target_pairs={{0,6},{2,0},{4,2},{6,4},{1,7},{3,1},{5,3},{7,5},{8,14},{10,8},{12,... | collective-permute-start | bytes 313352 | tf_op jit(solution)/shard_map/ppermute | solution.py:42
  117.3 6.2 %collective-permute-start.16 = (bf16[136,384]{1,0:T(8,128)(2,1)S(1)}, bf16[136,384]{1,0:T(8,128)(2,1)S(1)}, u32[]{:S(2)}, u32[]{:S(2)}) collective-permute-start(bf16[136,384]{1,0:T(8,128)(2,1)S(1)} %get-tuple-element.31), channel_id=1, source_target_pairs={{0,8},{8,16},{16,24},{24,0},{1,9},{9,17},{17,25},{25,1},{2,10},{10... | collective-permute-start | bytes 313352 | tf_op jit(solution)/shard_map/ppermute | solution.py:42
  117.4 6.1 %collective-permute-start.17 = (bf16[136,384]{1,0:T(8,128)(2,1)S(1)}, bf16[136,384]{1,0:T(8,128)(2,1)S(1)}, u32[]{:S(2)}, u32[]{:S(2)}) collective-permute-start(bf16[136,384]{1,0:T(8,128)(2,1)S(1)} %get-tuple-element.33), channel_id=1, source_target_pairs={{0,16},{8,24},{16,0},{24,8},{1,17},{9,25},{17,1},{25,9},{2,18},{10... | collective-permute-start | bytes 313352 | tf_op jit(solution)/shard_map/ppermute | solution.py:42
  119.8 4.3 %collective-permute-start.18 = (bf16[136,384]{1,0:T(8,128)(2,1)S(1)}, bf16[136,384]{1,0:T(8,128)(2,1)S(1)}, u32[]{:S(2)}, u32[]{:S(2)}) collective-permute-start(bf16[136,384]{1,0:T(8,128)(2,1)S(1)} %get-tuple-element.32), channel_id=1, source_target_pairs={{0,24},{8,0},{16,8},{24,16},{1,25},{9,1},{17,9},{25,17},{2,26},{10... | collective-permute-start | bytes 313352 | tf_op jit(solution)/shard_map/ppermute | solution.py:42
  124.4 35.9 %copy-start = (f32[256,384]{1,0:T(8,128)}, f32[256,384]{1,0:T(8,128)S(1)}, u32[]{:S(2)}) copy-start(f32[256,384]{1,0:T(8,128)S(1)} %get-tuple-element.25) | copy-start | bytes 1179652
